TPU v7x, 32 devices: a whole 2x2x4 slice. The times are simulated.
32 devices in a mesh: seq: 8 (over z, y), dp: 4 (over x, core).
Axes of the slice: x: 2, y: 2, z: 4, core: 2. Of those that a mesh axis runs over, the one named last changes fastest.
Arguments:
- queries: bfloat16 [4, 2048, 2048], P('dp', 'seq'), may hold values from -12 to 12
- keys: bfloat16 [4, 2048, 1024], P('dp', 'seq'), may hold values from -6 to 6
- values: bfloat16 [4, 2048, 1024], P('dp', 'seq'), may hold values from -6 to 6
- out_grad: bfloat16 [4, 2048, 1792], P('dp', 'seq'), may hold values from -6 to 6
- out_weight: bfloat16 [2048, 1792], P('seq'), may hold values from -0.125 to 0.125
- seq_len: int32 [4], P('dp'), may hold values from 512 to 2048, as said below
Outputs:
- query_grad: bfloat16 [4, 2048, 2048], P('dp', 'seq')
- key_grad: bfloat16 [4, 2048, 1024], P('dp', 'seq')
- value_grad: bfloat16 [4, 2048, 1024], P('dp', 'seq')
- weight_grad: float32 [2048, 1792], P('seq')
- grad_rms: float32 [], replicated
Inputs may be any that keep to these rules, and one draw needn't show every extreme that they name: `seq_len`: at least one sequence has the full length 2048.
All inputs are finite; a program needn't handle non-finite values.
Results may differ from a plain program's by a relative error of at most 0.014.
Values may be sent and summed in bfloat16 or wider, within the bound.
A program may use at most 128 MiB of HBM per device.

v0:
```python
import jax
import jax.numpy as jnp
from jax import lax
from jax.sharding import PartitionSpec as P

HEADS = 8
KV_HEADS = 4
HEAD_DIM = 256
D_OUT = 1792
WINDOW = 512
TOK_DEV = 256


SCALE = 0.0625
CAP = 50.0


def shifted(value, axis, steps):
    count = lax.axis_size(axis)
    initial, last = (max(0, -steps), min(count, count - steps))
    return lax.ppermute(value, axis, [(source, source + steps) for source in range(initial, last)])


def band_block(q_rows, k_rows, v_rows, g_rows, q_pos, k_pos):
    count = q_rows.shape[0]
    span = k_rows.shape[0]
    group = HEADS // KV_HEADS
    qh = q_rows.reshape(count, KV_HEADS, group, HEAD_DIM)
    kh = k_rows.reshape(span, KV_HEADS, HEAD_DIM)
    vh = v_rows.reshape(span, KV_HEADS, HEAD_DIM)
    gh = g_rows.reshape(count, KV_HEADS, group, HEAD_DIM)
    raw = jnp.einsum("tkgd,jkd->kgtj", qh, kh, preferred_element_type=jnp.float32) * SCALE
    capped = CAP * jnp.tanh(raw / CAP)
    allowed = (
        (k_pos[None, :] >= 0)
        & (k_pos[None, :] <= q_pos[:, None])
        & (k_pos[None, :] > q_pos[:, None] - WINDOW)
    )
    expo = jnp.where(allowed, jnp.exp(capped), jnp.zeros((), jnp.float32))
    probs = expo / jnp.sum(expo, axis=-1, keepdims=True)
    probs_b = probs.astype(jnp.bfloat16)
    attn = jnp.einsum("kgtj,jkd->tkgd", probs_b, vh, preferred_element_type=jnp.float32).astype(
        jnp.bfloat16
    )
    delta = jnp.einsum("tkgd,tkgd->kgt", gh, attn, preferred_element_type=jnp.float32)[..., None]
    dprob = jnp.einsum("tkgd,jkd->kgtj", gh, vh, preferred_element_type=jnp.float32)
    dscore = (probs * (dprob - delta) * (1.0 - (capped / CAP) ** 2) * SCALE).astype(jnp.bfloat16)
    dq = jnp.einsum("kgtj,jkd->tkgd", dscore, kh, preferred_element_type=jnp.float32).reshape(
        count, -1
    )
    dk = jnp.einsum("kgtj,tkgd->jkd", dscore, qh, preferred_element_type=jnp.float32).reshape(
        span, -1
    )
    dv = jnp.einsum("kgtj,tkgd->jkd", probs_b, gh, preferred_element_type=jnp.float32).reshape(
        span, -1
    )
    return (dq, dk, dv, attn.reshape(count, -1))


def shards(queries, keys, values, out_grad, out_weight, seq_len):
    q_rows = queries[0]
    k_rows = keys[0]
    v_rows = values[0]
    length = seq_len[0]
    seq_devices = lax.axis_size("seq")
    rep_devices = lax.axis_size("dp")
    start = lax.axis_index("seq") * TOK_DEV
    positions = start + jnp.arange(TOK_DEV, dtype=jnp.int32)
    valid = positions < length
    masked = jnp.where(valid[:, None], out_grad[0], jnp.zeros((), jnp.bfloat16))
    grad_attn = lax.dot_general(
        masked,
        lax.all_gather(out_weight, "seq", axis=0, tiled=True),
        (((1,), (1,)), ((), ())),
        preferred_element_type=jnp.float32,
    ).astype(jnp.bfloat16)
    reach = (WINDOW + TOK_DEV - 2) // TOK_DEV
    lead = reach * TOK_DEV
    key_parts = []
    val_parts = []
    for back in range(reach, 0, -1):
        earlier_k, earlier_v = shifted((k_rows, v_rows), "seq", back)
        key_parts.append(earlier_k)
        val_parts.append(earlier_v)
    key_block = jnp.concatenate(key_parts + [k_rows], 0)
    val_block = jnp.concatenate(val_parts + [v_rows], 0)
    k_pos = start - lead + jnp.arange(lead + TOK_DEV, dtype=jnp.int32)
    dq_raw, dk_all, dv_all, attn = band_block(
        q_rows, key_block, val_block, grad_attn, positions, k_pos
    )
    dk_raw = dk_all[lead:]
    dv_raw = dv_all[lead:]
    for back in range(1, reach + 1):
        first = (reach - back) * TOK_DEV
        later_k, later_v = (
            shifted(dk_all[first : first + TOK_DEV].astype(jnp.bfloat16), "seq", -back).astype(
                jnp.float32
            ),
            shifted(dv_all[first : first + TOK_DEV].astype(jnp.bfloat16), "seq", -back).astype(
                jnp.float32
            ),
        )
        dk_raw = dk_raw + later_k
        dv_raw = dv_raw + later_v
    width = HEADS * HEAD_DIM
    weight_raw = lax.psum_scatter(
        lax.dot_general(attn, masked, (((0,), (0,)), ((), ())), preferred_element_type=jnp.float32),
        ("seq", "dp"),
        scatter_dimension=0,
        tiled=True,
    )
    weight_sq = jnp.sum(weight_raw * weight_raw)
    own_count = jnp.clip(length - start, 0, TOK_DEV)
    slots = TOK_DEV * seq_devices * rep_devices
    entries = slots * (HEADS + 2 * KV_HEADS) * HEAD_DIM + width * D_OUT
    total = lax.psum(own_count, ("seq", "dp")).astype(jnp.float32)
    act_scale = slots / total
    weight_scale = lax.rsqrt(total)
    dq_s = dq_raw * act_scale
    dk_s = dk_raw * act_scale
    dv_s = dv_raw * act_scale
    local = (
        jnp.sum(dq_s * dq_s)
        + jnp.sum(dk_s * dk_s)
        + jnp.sum(dv_s * dv_s)
        + weight_sq * (weight_scale * weight_scale)
    )
    squares = lax.psum(local, ("seq", "dp"))
    grad_rms = jnp.sqrt(squares / entries)
    weight_grad = weight_raw * weight_scale
    weight_grad = lax.all_gather(weight_grad.astype(jnp.bfloat16), "dp", axis=0, tiled=True).astype(
        weight_grad.dtype
    )
    return (
        dq_s.astype(jnp.bfloat16)[None],
        dk_s.astype(jnp.bfloat16)[None],
        dv_s.astype(jnp.bfloat16)[None],
        weight_grad,
        grad_rms,
    )


def solution(mesh):
    in_specs = (
        P("dp", "seq", None),
        P("dp", "seq", None),
        P("dp", "seq", None),
        P("dp", "seq", None),
        P("seq", None),
        P("dp"),
    )
    out_specs = (
        P("dp", "seq", None),
        P("dp", "seq", None),
        P("dp", "seq", None),
        P("seq", None),
        P(),
    )
    return jax.shard_map(shards, mesh=mesh, in_specs=in_specs, out_specs=out_specs, check_vma=False)
```

profile of v0, /device:TPU:1, one launch (start us, length us, event | category | flops | bytes accessed | tf_op | source)
XLA Modules:
  0.0 421.9 jit_solution(5991975301664683336)
XLA Ops:
  8.0 1.2 copy.28
  9.2 4.8 %collective-permute-start.1 = (bf16[256,1024]{0,1:T(8,128)(2,1)S(1)}, bf16[256,1024]{0,1:T(8,128)(2,1)}, u32[]{:S(2)}, u32[]{:S(2)}) collective-permute-start(bf16[256,1024]{0,1:T(8,128)(2,1)S(1)} %bitcast.112), channel_id=1, source_target_pairs={{0,4},{4,8},{8,12},{12,16},{16,20},{20,24},{24,28},{1,5},{5,9},{9,... | collective-permute-start | bytes 1572872 | tf_op jit(solution)/shard_map/ppermute | solution.py:21
  14.0 3.2 collective-permute-start
  17.2 1.2 copy.34
  18.4 4.0 collective-permute-start.3
  22.4 2.4 collective-permute-start.2
  27.6 1.2 copy.31
  28.9 2.6 collective-permute-done
  31.5 1.2 copy.30
  32.8 12.0 %collective-permute-done.3 = bf16[256,1024]{0,1:T(8,128)(2,1)} collective-permute-done((bf16[256,1024]{0,1:T(8,128)(2,1)S(1)}, bf16[256,1024]{0,1:T(8,128)(2,1)}, u32[]{:S(2)}, u32[]{:S(2)}) %collective-permute-start.3) | collective-permute-done | bytes 524320 | tf_op jit(solution)/shard_map/ppermute | solution.py:21
  44.8 2.0 copy.37
  46.9 7.1 %collective-permute-done.2 = bf16[256,1024]{0,1:T(8,128)(2,1)} collective-permute-done((bf16[256,1024]{0,1:T(8,128)(2,1)S(1)}, bf16[256,1024]{0,1:T(8,128)(2,1)}, u32[]{:S(2)}, u32[]{:S(2)}) %collective-permute-start.2) | collective-permute-done | bytes 524320 | tf_op jit(solution)/shard_map/ppermute | solution.py:21
  54.0 2.1 copy.36
  56.1 2.0 fusion.4
  58.1 2.6 copy-done
  60.6 1.8 fusion.5
  62.5 88.0 %all-gather.2.cloned.1.call-done = bf16[2048,1792]{1,0:T(8,128)(2,1)} async-done(((bf16[256,1792]{1,0:T(8,128)(2,1)}), bf16[2048,1792]{1,0:T(8,128)(2,1)}) %all-gather.2.cloned.1.call-update) | async-done | bytes 7340048 | tf_op jit(solution)/shard_map/all_gather | solution.py:73
  150.5 6.5 %convolution_convert_fusion = bf16[256,2048]{1,0:T(8,128)(2,1)} fusion(bf16[2048,1792]{1,0:T(8,128)(2,1)} %all-gather.2.cloned.1.call-done, bf16[1,256,1792]{2,1,0:T(8,128)(2,1)} %param.9, pred[256]{0:T(512)(128)(4,1)S(1)} %fusion.15), kind=kOutput, calls=%fused_computation.10 | convolution fusion | flops 1880031232 | bytes 9306368 | tf_op jit(solution)/shard_map/dot_general | solution.py:71
  157.0 2.6 reshape.84
  159.6 3.3 bitcast_convert_fusion
  162.9 4.1 copy.64
  167.0 3.2 multiply_reduce_fusion
  170.2 7.3 %fusion.6 = f32[2048,1792]{1,0:T(8,128)} fusion(bf16[256,2048]{0,1:T(8,128)(2,1)S(1)} %bitcast.119, bf16[1,256,1792]{2,1,0:T(8,128)(2,1)S(1)} %copy-done.6, pred[256]{0:T(512)(128)(4,1)S(1)} %fusion.15), kind=kOutput, calls=%fused_computation.24 | convolution fusion | flops 1879506944 | bytes 16646400 | tf_op jit(solution)/shard_map/dot_general | solution.py:107
  177.6 45.3 %psum.14 = s32[]{:T(128)} all-reduce(s32[]{:T(128)S(6)} %min.4), channel_id=1, replica_groups=mesh['seq'=8,'dp'=4] {'seq','dp'}, use_global_device_ids=true, to_apply=%region_1.2 | all-reduce | flops 1 | bytes 8 | tf_op jit(solution)/shard_map/psum | solution.py:116
  223.7 3.7 copy.49
  227.3 6.9 %fusion.1 = bf16[4,2,256,768]{2,3,1,0:T(8,128)(2,1)S(1)} fusion(f32[4,768,256,2]{2,1,3,0:T(8,128)} %copy-done, f32[4,2,256]{2,1,0:T(2,128)S(1)} %get-tuple-element.29, f32[4,2,256]{2,1,0:T(2,128)S(1)} %get-tuple-element.27, pred[256,768]{0,1:T(8,128)(4,1)S(1)} %compare_and_fusion, bf16[256,4,2,256]{0,3,2,1:T(8,128)(2,1)} %copy.49, ...), kind=kOutput, calls=%fused_computation.2 | convolution fusion | flops 827326464 | bytes 12271616 | tf_op jit(solution)/shard_map/tkgd,jkd->kgtj/dot_general | solution.py:46
  234.3 2.6 fusion.25
  238.0 2.1 copy.48
  240.1 1.3 collective-permute-start.5
  241.4 2.1 copy.46
  243.4 1.3 collective-permute-start.4
  244.7 3.9 fusion.26
  249.6 2.3 copy.53
  252.0 1.3 collective-permute-start.7
  253.3 2.1 copy.51
  255.3 1.3 collective-permute-start.6
  256.6 4.0 multiply_reduce_fusion.1
  260.6 2.3 copy.54
  262.9 1.3 slice.40
  264.5 1.3 slice.43
  266.2 2.9 multiply_reduce_fusion.3
  270.4 26.9 %collective-permute-done.7 = bf16[256,1024]{1,0:T(8,128)(2,1)} collective-permute-done((bf16[256,1024]{1,0:T(8,128)(2,1)}, bf16[256,1024]{1,0:T(8,128)(2,1)}, u32[]{:S(2)}, u32[]{:S(2)}) %collective-permute-start.7) | collective-permute-done | bytes 524320 | tf_op jit(solution)/shard_map/ppermute | solution.py:21
  297.3 2.9 multiply_reduce_fusion.2
  300.8 47.8 %reduce-scatter.2.cloned.1.call-done = f32[64,1792]{1,0:T(8,128)} async-done(((f32[2048,1792]{1,0:T(8,128)}), f32[64,1792]{1,0:T(8,128)}) %reduce-scatter.2.cloned.1.call-update) | async-done | bytes 458768 | tf_op jit(solution)/shard_map/reduce_scatter | solution.py:106
  348.7 1.7 multiply_reduce_fusion.4
  350.4 14.0 %all_gather.7 = bf16[256,1792]{1,0:T(8,128)(2,1)S(1)} all-gather(bf16[64,1792]{1,0:T(8,128)(2,1)S(1)} %get-tuple-element.26), channel_id=1, replica_groups=mesh['seq'=8,'dp'=4] {'dp'}, dimensions={0}, use_global_device_ids=true | all-gather | bytes 1146880 | tf_op jit(solution)/shard_map/all_gather | solution.py:131
  365.1 1.3 convert_element_type.94
  366.4 46.9 %psum.15 = f32[]{:T(128)} all-reduce(f32[]{:T(128)S(6)} %add.73), channel_id=1, replica_groups=mesh['seq'=8,'dp'=4] {'seq','dp'}, use_global_device_ids=true, to_apply=%region_7.8 | all-reduce | flops 1 | bytes 8 | tf_op jit(solution)/shard_map/psum | solution.py:128
  (39 shorter events, 5.7 us)
Async XLA Ops:
  7.2 18.3 %copy-start.5 = (bf16[1,256,2048]{2,1,0:T(8,128)(2,1)S(1)}, bf16[1,256,2048]{2,1,0:T(8,128)(2,1)}, u32[]{:S(2)}) copy-start(bf16[1,256,2048]{2,1,0:T(8,128)(2,1)} %param.6) | copy-start | bytes 3145732
  7.2 143.3 %all-gather.2.cloned.1.call-start = ((), (), s32[]{:S(2)}) async-start(), calls=%async_computation.1 | async-start | bytes 8257536 | tf_op jit(solution)/shard_map/all_gather | solution.py:73
  7.9 340.7 %reduce-scatter.2.cloned.1.call-start = ((), (), s32[]{:S(2)}) async-start(), calls=%async_computation.2 | async-start | bytes 15138816 | tf_op jit(solution)/shard_map/reduce_scatter | solution.py:106
  9.2 18.4 %collective-permute-start.1 = (bf16[256,1024]{0,1:T(8,128)(2,1)S(1)}, bf16[256,1024]{0,1:T(8,128)(2,1)}, u32[]{:S(2)}, u32[]{:S(2)}) collective-permute-start(bf16[256,1024]{0,1:T(8,128)(2,1)S(1)} %bitcast.112), channel_id=1, source_target_pairs={{0,4},{4,8},{8,12},{12,16},{16,20},{20,24},{24,28},{1,5},{5,9},{9,... | collective-permute-start | bytes 1572872 | tf_op jit(solution)/shard_map/ppermute | solution.py:21
  14.0 17.6 %collective-permute-start = (bf16[256,1024]{0,1:T(8,128)(2,1)S(1)}, bf16[256,1024]{0,1:T(8,128)(2,1)}, u32[]{:S(2)}, u32[]{:S(2)}) collective-permute-start(bf16[256,1024]{0,1:T(8,128)(2,1)S(1)} %bitcast.113), channel_id=1, source_target_pairs={{0,8},{4,12},{8,16},{12,20},{16,24},{20,28},{1,9},{5,13},{9,17},{1... | collective-permute-start | bytes 1572872 | tf_op jit(solution)/shard_map/ppermute | solution.py:21
  18.4 26.4 %collective-permute-start.3 = (bf16[256,1024]{0,1:T(8,128)(2,1)S(1)}, bf16[256,1024]{0,1:T(8,128)(2,1)}, u32[]{:S(2)}, u32[]{:S(2)}) collective-permute-start(bf16[256,1024]{0,1:T(8,128)(2,1)S(1)} %bitcast.109), channel_id=1, source_target_pairs={{0,4},{4,8},{8,12},{12,16},{16,20},{20,24},{24,28},{1,5},{5,9},{9,... | collective-permute-start | bytes 1572872 | tf_op jit(solution)/shard_map/ppermute | solution.py:21
  22.4 31.6 %collective-permute-start.2 = (bf16[256,1024]{0,1:T(8,128)(2,1)S(1)}, bf16[256,1024]{0,1:T(8,128)(2,1)}, u32[]{:S(2)}, u32[]{:S(2)}) collective-permute-start(bf16[256,1024]{0,1:T(8,128)(2,1)S(1)} %bitcast.110), channel_id=1, source_target_pairs={{0,8},{4,12},{8,16},{12,20},{16,24},{20,28},{1,9},{5,13},{9,17},{1... | collective-permute-start | bytes 1572872 | tf_op jit(solution)/shard_map/ppermute | solution.py:21
  26.0 30.1 %copy-start.1 = (bf16[1,256,2048]{1,2,0:T(8,128)(2,1)}, bf16[1,256,2048]{1,2,0:T(8,128)(2,1)S(1)}, u32[]{:S(2)}) copy-start(bf16[1,256,2048]{1,2,0:T(8,128)(2,1)S(1)} %copy.75) | copy-start | bytes 3145732
  26.2 31.8 %copy-start.7 = (bf16[256,4,256]{2,0,1:T(8,128)(2,1)}, bf16[256,4,256]{2,0,1:T(8,128)(2,1)S(1)}, u32[]{:S(2)}) copy-start(bf16[256,4,256]{2,0,1:T(8,128)(2,1)S(1)} %copy.32) | copy-start | bytes 1572868
  28.9 29.2 %copy-start.8 = (bf16[256,4,256]{2,0,1:T(8,128)(2,1)}, bf16[256,4,256]{2,0,1:T(8,128)(2,1)S(1)}, u32[]{:S(2)}) copy-start(bf16[256,4,256]{2,0,1:T(8,128)(2,1)S(1)} %copy.31) | copy-start | bytes 1572868
  32.8 25.3 %copy-start.9 = (bf16[256,4,256]{2,0,1:T(8,128)(2,1)}, bf16[256,4,256]{2,0,1:T(8,128)(2,1)S(1)}, u32[]{:S(2)}) copy-start(bf16[256,4,256]{2,0,1:T(8,128)(2,1)S(1)} %copy.30) | copy-start | bytes 1572868
  58.1 2.6 copy-start
  167.0 3.2 copy-start.6
  227.3 6.9 %copy-start.2 = (bf16[1,256,2048]{1,2,0:T(8,128)(2,1)S(1)}, bf16[1,256,2048]{1,2,0:T(8,128)(2,1)}, u32[]{:S(2)}) copy-start(bf16[1,256,2048]{1,2,0:T(8,128)(2,1)} %copy-done.1) | copy-start | bytes 3145732
  234.3 2.7 copy-start.3
  240.1 26.1 %collective-permute-start.5 = (bf16[256,1024]{1,0:T(8,128)(2,1)}, bf16[256,1024]{1,0:T(8,128)(2,1)}, u32[]{:S(2)}, u32[]{:S(2)}) collective-permute-start(bf16[256,1024]{1,0:T(8,128)(2,1)} %copy.48), channel_id=1, source_target_pairs={{8,0},{12,4},{16,8},{20,12},{24,16},{28,20},{9,1},{13,5},{17,9},{2... | collective-permute-start | bytes 1572872 | tf_op jit(solution)/shard_map/ppermute | solution.py:21
  243.4 22.8 %collective-permute-start.4 = (bf16[256,1024]{1,0:T(8,128)(2,1)}, bf16[256,1024]{1,0:T(8,128)(2,1)}, u32[]{:S(2)}, u32[]{:S(2)}) collective-permute-start(bf16[256,1024]{1,0:T(8,128)(2,1)} %copy.46), channel_id=1, source_target_pairs={{4,0},{8,4},{12,8},{16,12},{20,16},{24,20},{28,24},{5,1},{9,5},{13... | collective-permute-start | bytes 1572872 | tf_op jit(solution)/shard_map/ppermute | solution.py:21
  248.6 8.0 %copy-start.4 = (bf16[4,2,256,768]{2,3,1,0:T(8,128)(2,1)S(1)}, bf16[4,2,256,768]{2,3,1,0:T(8,128)(2,1)}, u32[]{:S(2)}) copy-start(bf16[4,2,256,768]{2,3,1,0:T(8,128)(2,1)} %copy-done.3) | copy-start | bytes 9437188
  252.0 45.3 %collective-permute-start.7 = (bf16[256,1024]{1,0:T(8,128)(2,1)}, bf16[256,1024]{1,0:T(8,128)(2,1)}, u32[]{:S(2)}, u32[]{:S(2)}) collective-permute-start(bf16[256,1024]{1,0:T(8,128)(2,1)} %copy.53), channel_id=1, source_target_pairs={{8,0},{12,4},{16,8},{20,12},{24,16},{28,20},{9,1},{13,5},{17,9},{2... | collective-permute-start | bytes 1572872 | tf_op jit(solution)/shard_map/ppermute | solution.py:21
  255.3 42.0 %collective-permute-start.6 = (bf16[256,1024]{1,0:T(8,128)(2,1)}, bf16[256,1024]{1,0:T(8,128)(2,1)}, u32[]{:S(2)}, u32[]{:S(2)}) collective-permute-start(bf16[256,1024]{1,0:T(8,128)(2,1)} %copy.51), channel_id=1, source_target_pairs={{4,0},{8,4},{12,8},{16,12},{20,16},{24,20},{28,24},{5,1},{9,5},{13... | collective-permute-start | bytes 1572872 | tf_op jit(solution)/shard_map/ppermute | solution.py:21
Sparse Core Ops, SparseCore 0:
  10.2 140.2 all-gather.1
  177.7 170.9 reduce-scatter.1
where the time goes:
time: 425 us; the launch traced here: 422 us
  waiting for transfers between devices  185 us (44%)
  blocking collectives  106 us (25%)
  local copies, waits for them, and re-layouts  40.1 us (9%)
  matrix products  36.4 us (9%)
  between operations  20.2 us (5%)
  starting transfers between devices  19.5 us (5%)
  other arithmetic  14.2 us (3%)
    all_gather x1, waiting for transfers between devices, shards(): lax.all_gather(out_weight, 'seq', axis=0, tiled=True)  88 us
    ppermute x8, waiting for transfers between devices, shifted(): lax.ppermute(value, axis, [(source, source + steps) for source in range(i...  48.8 us
    reduce_scatter x1, waiting for transfers between devices, shards(): lax.psum_scatter(lax.dot_general(attn, masked, (((0,), (0,)), ((), ())),...  47.8 us
    psum x1, blocking collectives, shards(): squares = lax.psum(local, ('seq', 'dp'))  46.9 us
    psum x1, blocking collectives, shards(): total = lax.psum(own_count, ('seq', 'dp')).astype(jnp.float32)  45.3 us
    ppermute x8, starting transfers between devices, shifted(): lax.ppermute(value, axis, [(source, source + steps) for source in range(i...  19.5 us
    all_gather x1, blocking collectives, shards(): lax.all_gather(weight_grad.astype(jnp.bfloat16), 'dp', axis=0, tiled=True)  14 us
    unnamed x24, local copies, waits for them, and re-layouts  11.5 us
  transfers between devices with their start and end apart: 10, of which 6 were waited for; matrix products, arithmetic and copies ran while one was open for 14% of the time, Pallas kernels for 0%

commit v1 on v0

--- a/solution.py
+++ b/solution.py
@@ -1,6 +1,10 @@
+import functools
+
 import jax
 import jax.numpy as jnp
 from jax import lax
+from jax.experimental import pallas as pl
+from jax.experimental.pallas import tpu as pltpu
 from jax.sharding import PartitionSpec as P
 
 HEADS = 8
@@ -140,7 +144,7 @@
     )
 
 
-def solution(mesh):
+def plain_solution(mesh):
     in_specs = (
         P("dp", "seq", None),
         P("dp", "seq", None),
@@ -157,3 +161,500 @@
         P(),
     )
     return jax.shard_map(shards, mesh=mesh, in_specs=in_specs, out_specs=out_specs, check_vma=False)
+
+
+MESH = pl.DeviceIdType.MESH
+F32, BF16 = jnp.float32, jnp.bfloat16
+VMEM_LIMIT = 60 * 1024 * 1024
+
+
+class Place:
+    def __init__(self, n_seq):
+        self.n = n_seq
+        self.nz = n_seq // 2
+        self.seq = lax.axis_index("seq")
+        self.dp = lax.axis_index("dp")
+        self.z, self.y = self.seq // 2, self.seq % 2
+        self.core = self.dp % 2
+        self.turn = 1 - 2 * self.core
+        self.pos = self.z + self.y * (n_seq - 1 - 2 * self.z)
+
+    def ring(self, offset):
+        p = (self.pos + self.turn * offset + 4 * self.n) % self.n
+        far = p // self.nz
+        z = p + far * (self.n - 1 - 2 * p)
+        return 2 * z + far
+
+    def dp_flip(self, k):
+        if k == 1:
+            return self.dp + 1 - 2 * self.core
+        if k == 2:
+            return (self.dp + 2) % 4
+        return 3 - self.dp
+
+    def y_flip(self):
+        return self.seq + 1 - 2 * self.y
+
+
+def remote(src, dst, send, recv, seq, dp):
+    return pltpu.make_async_remote_copy(
+        src_ref=src, dst_ref=dst, send_sem=send, recv_sem=recv, device_id=(seq, dp), device_id_type=MESH
+    )
+
+
+def meet(peers):
+    barrier = pltpu.get_barrier_semaphore()
+    for seq, dp in peers:
+        pl.semaphore_signal(barrier, inc=1, device_id=(seq, dp), device_id_type=MESH)
+    pl.semaphore_wait(barrier, len(peers))
+
+
+def rows_at(first, count):
+    return pl.ds(pl.multiple_of(first, count), count)
+
+
+def gather_kernel(n_seq, w_ref, k_ref, v_ref, len_ref, w_full, k_halo, v_halo, total_ref,
+                  lens, zeros, ring_s, ring_r, x_s, x_r, c_s, c_r, cx_s, cx_r,
+                  z_s, z_r, y_s, y_r, l_s, l_r, own_sem):
+    at = Place(n_seq)
+    seq, dp, z, y, nz = at.seq, at.dp, at.z, at.y, at.nz
+    part = w_ref.shape[0]
+    quarter = part // 4
+    tok = k_ref.shape[0]
+    meet([(at.ring(1), dp), (at.ring(-1), dp), (at.y_flip(), dp)] + [(seq, at.dp_flip(k)) for k in (1, 2, 3)])
+
+    def piece(owner, q):
+        return w_full.at[rows_at(owner * part + q * quarter, quarter)]
+
+    steps = n_seq - 1
+
+    def ring_copy(t):
+        owner = at.ring(-t)
+        src = w_ref.at[rows_at(dp * quarter, quarter)] if t == 0 else piece(owner, dp)
+        return remote(src, piece(owner, dp), ring_s.at[t], ring_r.at[t], at.ring(1), dp)
+
+    def x_copy(t):
+        spot = piece(at.ring(-t - 1), dp)
+        return remote(spot, spot, x_s.at[t], x_r.at[t], seq, at.dp_flip(2))
+
+    def c_copy(t):
+        spot = piece(at.ring(-t - 1), dp)
+        return remote(spot, spot, c_s.at[t], c_r.at[t], seq, at.dp_flip(1))
+
+    def cx_copy(t):
+        spot = piece(at.ring(-t - 1), at.dp_flip(2))
+        return remote(spot, spot, cx_s.at[t], cx_r.at[t], seq, at.dp_flip(1))
+
+    blocks, halos = (k_ref, v_ref), (k_halo, v_halo)
+    up = jnp.minimum(seq + 2, n_seq - 1 - (1 - y))
+
+    def z_copy(i):
+        return remote(blocks[i], halos[i].at[pl.ds(0, tok)], z_s.at[i], z_r.at[i], up, dp)
+
+    def y_copy(i, relay):
+        src = halos[i].at[pl.ds(0, tok)] if relay else blocks[i]
+        return remote(src, halos[i].at[pl.ds(tok, tok)], y_s.at[i], y_r.at[i], at.y_flip(), dp)
+
+    ring = [ring_copy(t) for t in range(steps)]
+    xc = [x_copy(t) for t in range(steps)]
+    cc = [c_copy(t) for t in range(steps)]
+    cx = [cx_copy(t) for t in range(steps)]
+
+    len_copies = [remote(len_ref, lens.at[k - 1], l_s.at[k - 1], l_r.at[k - 1], seq, at.dp_flip(k)) for k in (1, 2, 3)]
+    ring[0].start()
+    for c in len_copies:
+        c.start()
+
+    @pl.when(z < nz - 1)
+    def _():
+        z_copy(0).start()
+
+    @pl.when(y == 0)
+    def _():
+        y_copy(0, False).start()
+        y_copy(1, False).start()
+
+    own = pltpu.make_async_copy(w_ref, w_full.at[rows_at(seq * part, part)], own_sem.at[0])
+    own.start()
+
+    @pl.when(z == 0)
+    def _():
+        zeros[...] = jnp.zeros_like(zeros)
+        for i in range(2):
+            c = pltpu.make_async_copy(zeros, halos[i].at[pl.ds(0, tok)], own_sem.at[1 + i])
+            c.start()
+            c.wait()
+
+        @pl.when(y == 0)
+        def _():
+            for i in range(2):
+                c = pltpu.make_async_copy(zeros, halos[i].at[pl.ds(tok, tok)], own_sem.at[1 + i])
+                c.start()
+                c.wait()
+
+    def relay(i):
+        @pl.when(z > 0)
+        def _():
+            z_copy(i).wait_recv()
+
+            @pl.when(y == 1)
+            def _():
+                y_copy(i, True).start()
+
+    for t in range(steps):
+        ring[t].wait_recv()
+        if t + 1 < steps:
+            ring[t + 1].start()
+        xc[t].start()
+        cc[t].start()
+        if t > 0:
+            xc[t - 1].wait_recv()
+            cx[t - 1].start()
+        if t == 2:
+            @pl.when(z < nz - 1)
+            def _():
+                z_copy(1).start()
+        if t == 3:
+            relay(0)
+    relay(1)
+    xc[steps - 1].wait_recv()
+    cx[steps - 1].start()
+    for c in len_copies:
+        c.wait()
+    total_ref[...] = len_ref[...] + lens[0] + lens[1] + lens[2]
+    for t in range(steps):
+        cc[t].wait_recv()
+        cx[t].wait_recv()
+
+    @pl.when((y == 1) | (z > 0))
+    def _():
+        for i in range(2):
+            y_copy(i, False).wait_recv()
+
+    @pl.when((y == 0) | (z > 0))
+    def _():
+        for i in range(2):
+            y_copy(i, False).wait_send()
+
+    @pl.when(z < nz - 1)
+    def _():
+        for i in range(2):
+            z_copy(i).wait_send()
+
+    own.wait()
+    for t in range(steps):
+        ring[t].wait_send()
+        xc[t].wait_send()
+        cc[t].wait_send()
+        cx[t].wait_send()
+
+
+def dot_t(a, b):
+    return lax.dot_general(a, b, (((1,), (1,)), ((), ())), preferred_element_type=F32)
+
+
+def dot_0(a, b):
+    return lax.dot_general(a, b, (((0,), (0,)), ((), ())), preferred_element_type=F32)
+
+
+def dot_n(a, b):
+    return lax.dot_general(a, b, (((1,), (0,)), ((), ())), preferred_element_type=F32)
+
+
+def tile_sum(x):
+    r, c = x.shape
+    s = jnp.sum(x.reshape(r // 8, 8, c), axis=0)
+    out = s[:, 0:128]
+    for j in range(1, c // 128):
+        out = out + s[:, j * 128 : (j + 1) * 128]
+    return out
+
+
+def attend_kernel(group, info_ref, act_ref, q_ref, k_ref, v_ref, kh_ref, vh_ref, g_ref, w_ref,
+                  dq_ref, dk_ref, dv_ref, dkh_ref, dvh_ref, wg_ref, sq_ref, masked_ref):
+    start, length = info_ref[0], info_ref[1]
+    tok, dim = k_ref.shape
+    lead = kh_ref.shape[0]
+    span = lead + tok
+    act = act_ref[0, 0]
+
+    @pl.when(pl.program_id(0) == 0)
+    def _():
+        row = start + lax.broadcasted_iota(jnp.int32, (tok, 1), 0)
+        masked_ref[...] = jnp.where(row < length, g_ref[...].astype(F32), 0.0).astype(BF16)
+        sq_ref[...] = jnp.zeros_like(sq_ref)
+
+    masked = masked_ref[...]
+    kc = jnp.concatenate([kh_ref[...], k_ref[...]], 0)
+    vc = jnp.concatenate([vh_ref[...], v_ref[...]], 0)
+    qi = lax.broadcasted_iota(jnp.int32, (tok, span), 0)
+    kj = lax.broadcasted_iota(jnp.int32, (tok, span), 1) - lead
+    allowed = (kj <= qi) & (kj > qi - WINDOW) & (kj + start >= 0)
+    dk = dv = None
+    for h in range(group):
+        cols = slice(h * dim, (h + 1) * dim)
+        qh = q_ref[:, cols]
+        gh = dot_t(masked, w_ref[cols, :]).astype(BF16)
+        t = jnp.tanh(dot_t(qh, kc) * (SCALE / CAP))
+        e = jnp.where(allowed, jnp.exp(CAP * t), 0.0)
+        p = e * (1.0 / jnp.sum(e, axis=-1, keepdims=True))
+        pb = p.astype(BF16)
+        attn = dot_n(pb, vc).astype(BF16)
+        delta = jnp.sum(gh.astype(F32) * attn.astype(F32), axis=-1, keepdims=True)
+        ds = (p * (dot_t(gh, vc) - delta) * ((1.0 - t * t) * SCALE)).astype(BF16)
+        dq = dot_n(ds, kc) * act
+        dq_ref[:, cols] = dq.astype(BF16)
+        sq_ref[...] += tile_sum(dq * dq)
+        dkh = dot_0(ds, qh)
+        dvh = dot_0(pb, gh)
+        dk = dkh if dk is None else dk + dkh
+        dv = dvh if dv is None else dv + dvh
+        wg_ref[cols, :] = dot_0(attn, masked).astype(BF16)
+    dk_ref[...] = dk[lead:]
+    dv_ref[...] = dv[lead:]
+    dkh_ref[...] = dk[:lead].astype(BF16)
+    dvh_ref[...] = dv[:lead].astype(BF16)
+
+
+def reduce_kernel(n_seq, entries, wg_ref, dk_ref, dv_ref, dkh_ref, dvh_ref, sq_ref, total_ref,
+                  kg_ref, vg_ref, wgrad_ref, rms_ref,
+                  cbuf, xsend, xbuf, rsend, rbuf, gown, gbuf, ybuf, zbuf, zsend, s_own, s_in, s_mid, s_all,
+                  c_s, c_r, x_s, x_r, r_s, r_r, g_s, g_r, y_s, y_r, z_s, z_r, a_s, a_r, b_s, b_r):
+    at = Place(n_seq)
+    seq, dp, z, y, nz = at.seq, at.dp, at.z, at.y, at.nz
+    part = wg_ref.shape[0] // n_seq
+    half, quarter = part // 2, part // 4
+    tok = dk_ref.shape[0]
+    x = dp // 2
+    meet(
+        [(at.ring(1), dp), (at.ring(-1), dp), (at.y_flip(), dp)]
+        + [(seq, at.dp_flip(k)) for k in (1, 2, 3)]
+        + [((seq + k) % n_seq, dp) for k in range(1, n_seq)]
+    )
+    def quarter_row(d):
+        return (d % 2) * half + (d // 2) * quarter
+
+    def c_copy(u):
+        owner = at.ring(u + 1)
+        src = wg_ref.at[rows_at(owner * part + (1 - at.core) * half, half)]
+        return remote(src, cbuf.at[u], c_s.at[u], c_r.at[u], seq, at.dp_flip(1))
+
+    cc = [c_copy(u) for u in range(n_seq)]
+    xc = [remote(xsend.at[u], xbuf.at[u], x_s.at[u], x_r.at[u], seq, at.dp_flip(2)) for u in range(n_seq)]
+    rc = [remote(rsend.at[u], rbuf.at[u], r_s.at[u], r_r.at[u], at.ring(1), dp) for u in range(n_seq - 1)]
+    halos = (dkh_ref, dvh_ref)
+    down = jnp.maximum(seq - 2, y)
+
+    def y_copy(i):
+        return remote(halos[i].at[pl.ds(tok, tok)], ybuf.at[i], y_s.at[i], y_r.at[i], at.y_flip(), dp)
+
+    def z_copy(i, summed):
+        src = zsend.at[i] if summed else halos[i].at[pl.ds(0, tok)]
+        return remote(src, zbuf.at[i], z_s.at[i], z_r.at[i], down, dp)
+
+    for u in range(n_seq):
+        cc[u].start()
+
+    @pl.when((y == 1) | (z > 0))
+    def _():
+        for i in range(2):
+            y_copy(i).start()
+
+    @pl.when((y == 0) & (z > 0))
+    def _():
+        for i in range(2):
+            z_copy(i, False).start()
+
+    for u in range(n_seq):
+        cc[u].wait_recv()
+        first = at.ring(-u - 1) * part + at.core * half + (1 - x) * quarter
+        mine = wg_ref[rows_at(first, quarter), :].astype(F32)
+        theirs = cbuf[u, rows_at((1 - x) * quarter, quarter), :].astype(F32)
+        xsend[u] = (mine + theirs).astype(BF16)
+        xc[u].start()
+
+    def chunk(u):
+        first = at.ring(-u - 1) * part + at.core * half + x * quarter
+        acc = wg_ref[rows_at(first, quarter), :].astype(F32)
+        acc = acc + cbuf[u, rows_at(x * quarter, quarter), :].astype(F32)
+        xc[u].wait_recv()
+        acc = acc + xbuf[u].astype(F32)
+        if u > 0:
+            rc[u - 1].wait_recv()
+            acc = acc + rbuf[u - 1].astype(F32)
+        return acc
+
+    def relay(i):
+        @pl.when((y == 0) | (z > 0))
+        def _():
+            y_copy(i).wait_recv()
+
+        @pl.when((y == 1) & (z > 0))
+        def _():
+            zsend[i] = (halos[i][0:tok, :].astype(F32) + ybuf[i].astype(F32)).astype(BF16)
+            z_copy(i, True).start()
+
+    for u in range(n_seq - 1):
+        rsend[u] = chunk(u).astype(BF16)
+        rc[u].start()
+        if u == 1:
+            relay(0)
+        if u == 3:
+            relay(1)
+
+    total = total_ref[0:1, 0:1]
+    act = (tok * n_seq * 4) / total
+    wscale = lax.rsqrt(total)
+    grads = []
+    square = sq_ref[...]
+    for i, (own, out) in enumerate(((dk_ref, kg_ref), (dv_ref, vg_ref))):
+        @pl.when(z < nz - 1)
+        def _():
+            z_copy(i, False).wait_recv()
+
+        val = own[...]
+        val = val + jnp.where(y == 0, ybuf[i].astype(F32), 0.0)
+        val = val + jnp.where(z < nz - 1, zbuf[i].astype(F32), 0.0)
+        val = val * act
+        out[...] = val.astype(BF16)
+        square = square + tile_sum(val * val)
+
+    raw = chunk(n_seq - 1)
+    gown[...] = raw.astype(BF16)
+    gc = [remote(gown, gbuf.at[k - 1], g_s.at[k - 1], g_r.at[k - 1], seq, at.dp_flip(k)) for k in (1, 2, 3)]
+    scaled = raw * wscale
+    s_own[...] = square + tile_sum(scaled * scaled)
+    ac = [remote(s_own, s_in.at[k - 1], a_s.at[k - 1], a_r.at[k - 1], seq, at.dp_flip(k)) for k in (1, 2, 3)]
+    for c in ac:
+        c.start()
+    for c in gc:
+        c.start()
+    for c in ac:
+        c.wait_recv()
+    s_mid[...] = (s_own[...] + s_in[1]) + (s_in[0] + s_in[2])
+    bc = [
+        remote(s_mid, s_all.at[k - 1], b_s.at[k - 1], b_r.at[k - 1], (seq + k) % n_seq, dp)
+        for k in range(1, n_seq)
+    ]
+    for c in bc:
+        c.start()
+    wgrad_ref[rows_at(quarter_row(dp), quarter), :] = gown[...].astype(F32) * wscale
+    for k in (1, 2, 3):
+        gc[k - 1].wait_recv()
+        wgrad_ref[rows_at(quarter_row(at.dp_flip(k)), quarter), :] = gbuf[k - 1].astype(F32) * wscale
+    for c in bc:
+        c.wait_recv()
+    final = s_mid[...]
+    for k in range(n_seq - 1):
+        final = final + s_all[k]
+    whole = jnp.sum(jnp.sum(final, axis=1, keepdims=True), axis=0, keepdims=True)
+    rms_ref[...] = jnp.broadcast_to(jnp.sqrt(whole / entries), rms_ref.shape)
+
+    for c in cc + xc + rc + gc + ac + bc:
+        c.wait_send()
+
+    @pl.when((y == 1) | (z > 0))
+    def _():
+        for i in range(2):
+            y_copy(i).wait_send()
+
+    @pl.when(z > 0)
+    def _():
+        for i in range(2):
+            z_copy(i, False).wait_send()
+
+
+ANY = pl.BlockSpec(memory_space=pl.ANY)
+VM = pl.BlockSpec(memory_space=pltpu.VMEM)
+DMA = pltpu.SemaphoreType.DMA
+
+
+def fast_shards(n_seq, queries, keys, values, out_grad, out_weight, seq_len):
+    q, k, v, g = queries[0], keys[0], values[0], out_grad[0]
+    tok, kv_width = k.shape
+    part, d_out = out_weight.shape
+    width = part * n_seq
+    dim, group = HEAD_DIM, HEADS // KV_HEADS
+    lead = 2 * tok
+    steps = n_seq - 1
+    sds = jax.ShapeDtypeStruct
+    length = jnp.clip(seq_len[0], 0, tok * n_seq)
+    len_tile = jnp.full((8, 128), length.astype(F32), F32)
+    w_full, k_halo, v_halo, total = pl.pallas_call(
+        functools.partial(gather_kernel, n_seq),
+        out_shape=(sds((width, d_out), BF16), sds((lead, kv_width), BF16), sds((lead, kv_width), BF16), sds((8, 128), F32)),
+        in_specs=[VM] * 4,
+        out_specs=(ANY, ANY, ANY, VM),
+        scratch_shapes=[pltpu.VMEM((3, 8, 128), F32), pltpu.VMEM((tok, kv_width), BF16)]
+        + [DMA((steps,))] * 8 + [DMA((2,))] * 4 + [DMA((3,))] * 3,
+        compiler_params=pltpu.CompilerParams(collective_id=0, has_side_effects=True, vmem_limit_bytes=VMEM_LIMIT // 2),
+    )(out_weight, k, v, len_tile)
+    start = lax.axis_index("seq").astype(jnp.int32) * tok
+    info = jnp.stack([start, seq_len[0]])
+    act = (tok * n_seq * 4) / total[0:1, 0:1]
+    smem = pl.BlockSpec(memory_space=pltpu.SMEM)
+
+    def col(rows, cols):
+        return pl.BlockSpec((rows, cols), lambda i: (0, i))
+
+    dq, dk, dv, dkh, dvh, wg, sq = pl.pallas_call(
+        functools.partial(attend_kernel, group),
+        grid=(KV_HEADS,),
+        out_shape=(
+            sds((tok, width), BF16), sds((tok, kv_width), F32), sds((tok, kv_width), F32),
+            sds((lead, kv_width), BF16), sds((lead, kv_width), BF16), sds((width, d_out), BF16), sds((8, 128), F32),
+        ),
+        in_specs=[
+            smem, smem, col(tok, group * dim), col(tok, dim), col(tok, dim), col(lead, dim), col(lead, dim),
+            pl.BlockSpec((tok, d_out), lambda i: (0, 0)), pl.BlockSpec((group * dim, d_out), lambda i: (i, 0)),
+        ],
+        out_specs=(
+            col(tok, group * dim), col(tok, dim), col(tok, dim), col(lead, dim), col(lead, dim),
+            pl.BlockSpec((group * dim, d_out), lambda i: (i, 0)), pl.BlockSpec((8, 128), lambda i: (0, 0)),
+        ),
+        scratch_shapes=[pltpu.VMEM((tok, d_out), BF16)],
+        compiler_params=pltpu.CompilerParams(dimension_semantics=("arbitrary",), vmem_limit_bytes=VMEM_LIMIT),
+    )(info, act, q, k, v, k_halo, v_halo, g, w_full)
+    entries = tok * n_seq * 4 * (HEADS + 2 * KV_HEADS) * HEAD_DIM + width * d_out
+    quarter = part // 4
+    kg, vg, wgrad, rms = pl.pallas_call(
+        functools.partial(reduce_kernel, n_seq, float(entries)),
+        out_shape=(sds((tok, kv_width), BF16), sds((tok, kv_width), BF16), sds((part, d_out), F32), sds((8, 128), F32)),
+        in_specs=[VM] * 7,
+        out_specs=(VM,) * 4,
+        scratch_shapes=[
+            pltpu.VMEM((n_seq, part // 2, d_out), BF16),
+            pltpu.VMEM((n_seq, quarter, d_out), BF16),
+            pltpu.VMEM((n_seq, quarter, d_out), BF16),
+            pltpu.VMEM((steps, quarter, d_out), BF16),
+            pltpu.VMEM((steps, quarter, d_out), BF16),
+            pltpu.VMEM((quarter, d_out), BF16),
+            pltpu.VMEM((3, quarter, d_out), BF16),
+            pltpu.VMEM((2, tok, kv_width), BF16),
+            pltpu.VMEM((2, tok, kv_width), BF16),
+            pltpu.VMEM((2, tok, kv_width), BF16),
+            pltpu.VMEM((8, 128), F32),
+            pltpu.VMEM((3, 8, 128), F32),
+            pltpu.VMEM((8, 128), F32),
+            pltpu.VMEM((steps, 8, 128), F32),
+            DMA((n_seq,)), DMA((n_seq,)), DMA((n_seq,)), DMA((n_seq,)), DMA((steps,)), DMA((steps,)),
+            DMA((3,)), DMA((3,)), DMA((2,)), DMA((2,)), DMA((2,)), DMA((2,)),
+            DMA((3,)), DMA((3,)), DMA((steps,)), DMA((steps,)),
+        ],
+        compiler_params=pltpu.CompilerParams(collective_id=1, has_side_effects=True, vmem_limit_bytes=VMEM_LIMIT),
+    )(wg, dk, dv, dkh, dvh, sq, total)
+    return dq[None], kg[None], vg[None], wgrad, rms[0, 0]
+
+
+def solution(mesh):
+    n_seq, n_dp = mesh.shape["seq"], mesh.shape["dp"]
+    if n_seq != HEADS or n_dp != 4:
+        return plain_solution(mesh)
+    row = P("dp", "seq", None)
+    return jax.shard_map(
+        functools.partial(fast_shards, n_seq),
+        mesh=mesh,
+        in_specs=(row, row, row, row, P("seq", None), P("dp")),
+        out_specs=(row, row, row, P("seq", None), P()),
+        check_vma=False,
+    )

time: 425 us -> 189 us (0.44)
  waiting for transfers between devices: 185 us -> 0 us
  Pallas kernels: 0 us -> 170 us
  blocking collectives: 106 us -> 0 us
  matrix products: 36.4 us -> 0 us
  local copies, waits for them, and re-layouts: 40.1 us -> 16.5 us
  starting transfers between devices: 19.5 us -> 0 us
  between operations: 20.2 us -> 2.02 us
  other arithmetic: 14.2 us -> 0.58 us
    pallas_call x0 -> x3, Pallas kernels: none -> 170 us  [the longest x1 90.6 us: fast_shards(): pl.pallas_call(functools.partial(reduce_kernel, n_seq, float(entries)), o...]
    psum x2 -> x0, blocking collectives: 92.2 us -> none  [the longest x1 46.9 us: shards(): squares = lax.psum(local, ('seq', 'dp'))]
    all_gather x1 -> x0, waiting for transfers between devices: 88 us -> none  [shards(): lax.all_gather(out_weight, 'seq', axis=0, tiled=True)]
    ppermute x8 -> x0, waiting for transfers between devices: 48.8 us -> none  [shifted(): lax.ppermute(value, axis, [(source, source + steps) for source in range(i...]
    reduce_scatter x1 -> x0, waiting for transfers between devices: 47.8 us -> none  [shards(): lax.psum_scatter(lax.dot_general(attn, masked, (((0,), (0,)), ((), ())),...]
    dot_general x8 -> x0, matrix products: 36.4 us -> none  [the longest x1 7.35 us: shards(): lax.dot_general(attn, masked, (((0,), (0,)), ((), ())), preferred_element...]
    ppermute x8 -> x0, starting transfers between devices: 19.5 us -> none  [shifted(): lax.ppermute(value, axis, [(source, source + steps) for source in range(i...]
    all_gather x1 -> x0, blocking collectives: 14 us -> none  [shards(): lax.all_gather(weight_grad.astype(jnp.bfloat16), 'dp', axis=0, tiled=True)]
  transfers between devices with their start and end apart: 10 -> 0, of which waited for: 6 -> 0; matrix products, arithmetic and copies ran while one was open for 14% -> 0% of each run, Pallas kernels for 0% -> 0%
where the time goes in v1:
time: 189 us
  Pallas kernels  170 us (90%)
  local copies, waits for them, and re-layouts  16.5 us (9%)
  between operations  2.02 us (1%)
    pallas_call x1, Pallas kernels, fast_shards(): pl.pallas_call(functools.partial(reduce_kernel, n_seq, float(entries)), o...  90.6 us
    pallas_call x1, Pallas kernels, fast_shards(): pl.pallas_call(functools.partial(gather_kernel, n_seq), out_shape=(sds((w...  63.2 us
    pallas_call x1, Pallas kernels, fast_shards(): pl.pallas_call(functools.partial(attend_kernel, group), grid=(KV_HEADS,),...  15.9 us
    unnamed x17, local copies, waits for them, and re-layouts  14.8 us

profile of v1, /device:TPU:1, one launch (start us, length us, event | category | flops | bytes accessed | tf_op | source)
XLA Modules:
  0.0 188.8 jit_solution(10442993509846268698)
XLA Ops:
  1.3 0.6 pad_add_fusion.info_ref
  1.9 0.0 copy-start.1
  1.9 1.0 copy-done.1
  2.9 0.0 copy-start.2
  2.9 1.0 copy-done.2
  4.0 0.0 copy-start.5
  4.0 1.2 copy-done.5
  5.1 63.2 %shard_map.101 = (bf16[2048,1792]{1,0:T(8,128)(2,1)S(1)}, bf16[512,1024]{1,0:T(8,128)(2,1)S(1)}, bf16[512,1024]{1,0:T(8,128)(2,1)S(1)}, f32[8,128]{1,0:T(8,128)S(1)}) custom-call(bf16[256,1792]{1,0:T(8,128)(2,1)S(1)} %copy-done.5, bf16[256,1024]{1,0:T(8,128)(2,1)S(1)} %bitcast.11, bf16[256,1024]{1,0:T(8,128)(2,1)S(1)} %bitcast.13, ...), custom_call_target="tpu_custom_call" | custom-call | tf_op jit(solution)/shard_map/pallas_call | solution.py:583
  68.3 0.0 copy-start
  68.3 3.0 %copy-done = bf16[2048,1792]{1,0:T(8,128)(2,1)} copy-done((bf16[2048,1792]{1,0:T(8,128)(2,1)}, bf16[2048,1792]{1,0:T(8,128)(2,1)S(1)}, u32[]{:S(2)}) %copy-start) | copy-done | bytes 7340056
  71.3 0.0 copy-start.3
  71.3 1.0 copy-done.3
  72.3 0.0 copy-start.4
  72.3 1.0 copy-done.4
  73.3 0.0 copy-start.6
  73.3 0.5 slice.6
  74.5 15.9 %shard_map.102 = (bf16[256,2048]{1,0:T(8,128)(2,1)}, f32[256,1024]{1,0:T(8,128)}, f32[256,1024]{1,0:T(8,128)}, bf16[512,1024]{1,0:T(8,128)(2,1)}, bf16[512,1024]...) custom-call(s32[2]{0:T(128)} %pad_add_fusion.info_ref, f32[1,1]{1,0:T(1,128)S(6)} %div.3.act_ref, ...), custom_call_target="tpu_custom_call" | custom-call | tf_op jit(solution)/shard_map/pallas_call | solution.py:600
  90.4 0.0 copy-done.6
  90.4 90.6 %shard_map.103 = (bf16[256,1024]{1,0:T(8,128)(2,1)}, bf16[256,1024]{1,0:T(8,128)(2,1)}, f32[256,1792]{1,0:T(8,128)}, f32[8,128]{1,0:T(8,128)}) custom-call(bf16[2048,1792]{1,0:T(8,128)(2,1)} %get-tuple-element.25.wg_ref, f32[256,1024]{1,0:T(8,128)} %get-tuple-element.26.dk_ref, f32[256,1024]{1,0:T(8,128)} %get-tuple-element.27.dv_ref, ...), custom_call_target="tpu_custom_call" | custom-call | tf_op jit(solution)/shard_map/pallas_call | solution.py:620
  181.0 1.2 slice.7
  182.2 1.9 copy.15
  184.1 1.9 copy.16
  185.9 2.8 %copy.17 = f32[256,1792]{1,0:T(8,128)} copy(f32[256,1792]{1,0:T(8,128)} %get-tuple-element.43) | data formatting | bytes 3670016
  (1 shorter events, 0.0 us)
Async XLA Ops:
  1.9 1.0 copy-start.1
  2.9 1.0 copy-start.2
  4.0 1.2 copy-start.5
  68.3 3.0 %copy-start = (bf16[2048,1792]{1,0:T(8,128)(2,1)}, bf16[2048,1792]{1,0:T(8,128)(2,1)S(1)}, u32[]{:S(2)}) copy-start(bf16[2048,1792]{1,0:T(8,128)(2,1)S(1)} %get-tuple-element.23.w_ref) | copy-start | bytes 22020100
  71.3 1.0 copy-start.3
  72.3 1.0 copy-start.4
  73.3 17.1 %copy-start.6 = (f32[8,128]{1,0:T(8,128)}, f32[8,128]{1,0:T(8,128)S(1)}, u32[]{:S(2)}) copy-start(f32[8,128]{1,0:T(8,128)S(1)} %get-tuple-element.20.total_ref) | copy-start | bytes 12292

commit v2 on v1

--- a/solution.py
+++ b/solution.py
@@ -165,7 +165,7 @@
 
 MESH = pl.DeviceIdType.MESH
 F32, BF16 = jnp.float32, jnp.bfloat16
-VMEM_LIMIT = 60 * 1024 * 1024
+VMEM_LIMIT = 67043328
 
 
 class Place:
@@ -583,11 +583,11 @@
     w_full, k_halo, v_halo, total = pl.pallas_call(
         functools.partial(gather_kernel, n_seq),
         out_shape=(sds((width, d_out), BF16), sds((lead, kv_width), BF16), sds((lead, kv_width), BF16), sds((8, 128), F32)),
-        in_specs=[VM] * 4,
+        in_specs=[VM, ANY, ANY, VM],
         out_specs=(ANY, ANY, ANY, VM),
         scratch_shapes=[pltpu.VMEM((3, 8, 128), F32), pltpu.VMEM((tok, kv_width), BF16)]
         + [DMA((steps,))] * 8 + [DMA((2,))] * 4 + [DMA((3,))] * 3,
-        compiler_params=pltpu.CompilerParams(collective_id=0, has_side_effects=True, vmem_limit_bytes=VMEM_LIMIT // 2),
+        compiler_params=pltpu.CompilerParams(collective_id=0, has_side_effects=True, vmem_limit_bytes=VMEM_LIMIT),
     )(out_weight, k, v, len_tile)
     start = lax.axis_index("seq").astype(jnp.int32) * tok
     info = jnp.stack([start, seq_len[0]])

time: 189 us -> 185 us (0.979)
  local copies, waits for them, and re-layouts: 16.5 us -> 9.55 us
  Pallas kernels: 170 us -> 172 us
    unnamed x17 -> x3, local copies, waits for them, and re-layouts: 14.8 us -> 6.58 us
    pallas_call x1, Pallas kernels: 63.2 us -> 67.2 us  [fast_shards(): pl.pallas_call(functools.partial(gather_kernel, n_seq), out_shape=(sds((w...]
where the time goes in v2:
time: 185 us
  Pallas kernels  172 us (93%)
  local copies, waits for them, and re-layouts  9.55 us (5%)
  between operations  2 us (1%)
    pallas_call x1, Pallas kernels, fast_shards(): pl.pallas_call(functools.partial(reduce_kernel, n_seq, float(entries)), o...  89.2 us
    pallas_call x1, Pallas kernels, fast_shards(): pl.pallas_call(functools.partial(gather_kernel, n_seq), out_shape=(sds((w...  67.2 us
    pallas_call x1, Pallas kernels, fast_shards(): pl.pallas_call(functools.partial(attend_kernel, group), grid=(KV_HEADS,),...  15.9 us
    unnamed x3, local copies, waits for them, and re-layouts  6.58 us

profile of v2, /device:TPU:1, one launch (start us, length us, event | category | flops | bytes accessed | tf_op | source)
XLA Modules:
  0.0 184.6 jit_solution(3348017931587080194)
XLA Ops:
  1.3 0.6 pad_add_fusion.info_ref
  1.9 0.6 broadcast_in_dim.12.len_ref
  2.5 67.2 %shard_map.101 = (bf16[2048,1792]{1,0:T(8,128)(2,1)}, bf16[512,1024]{1,0:T(8,128)(2,1)}, bf16[512,1024]{1,0:T(8,128)(2,1)}, f32[8,128]{1,0:T(8,128)}) custom-call(bf16[256,1792]{1,0:T(8,128)(2,1)} %w_ref.1, bf16[256,1024]{1,0:T(8,128)(2,1)} %bitcast.10, bf16[256,1024]{1,0:T(8,128)(2,1)} %bitcast.12, f32[8,128]{1,0:T(8,128)} %broadcast_in_dim.12.len_ref), custom_call_target="tpu_custom_call" | custom-call | tf_op jit(solution)/shard_map/pallas_call | solution.py:583
  69.7 1.2 slice.6
  71.6 15.9 %shard_map.102 = (bf16[256,2048]{1,0:T(8,128)(2,1)}, f32[256,1024]{1,0:T(8,128)}, f32[256,1024]{1,0:T(8,128)}, bf16[512,1024]{1,0:T(8,128)(2,1)}, bf16[512,1024]...) custom-call(s32[2]{0:T(128)} %pad_add_fusion.info_ref, f32[1,1]{1,0:T(1,128)S(6)} %div.3.act_ref, ...), custom_call_target="tpu_custom_call" | custom-call | tf_op jit(solution)/shard_map/pallas_call | solution.py:600
  87.5 89.2 %shard_map.103 = (bf16[256,1024]{1,0:T(8,128)(2,1)}, bf16[256,1024]{1,0:T(8,128)(2,1)}, f32[256,1792]{1,0:T(8,128)}, f32[8,128]{1,0:T(8,128)}) custom-call(bf16[2048,1792]{1,0:T(8,128)(2,1)} %get-tuple-element.25.wg_ref, f32[256,1024]{1,0:T(8,128)} %get-tuple-element.26.dk_ref, f32[256,1024]{1,0:T(8,128)} %get-tuple-element.27.dv_ref, ...), custom_call_target="tpu_custom_call" | custom-call | tf_op jit(solution)/shard_map/pallas_call | solution.py:620
  176.8 1.2 slice.7
  178.0 1.9 %copy.15 = bf16[1,256,1024]{2,1,0:T(8,128)(2,1)} copy(bf16[1,256,1024]{2,1,0:T(8,128)(2,1)} %bitcast.17) | data formatting | bytes 1048576
  179.9 1.9 %copy.16 = bf16[1,256,1024]{2,1,0:T(8,128)(2,1)} copy(bf16[1,256,1024]{2,1,0:T(8,128)(2,1)} %bitcast.16) | data formatting | bytes 1048576
  181.7 2.8 %copy.17 = f32[256,1792]{1,0:T(8,128)} copy(f32[256,1792]{1,0:T(8,128)} %get-tuple-element.43) | data formatting | bytes 3670016
